TPU v7x, 32 devices: a 4x4x1 block of a 4x4x8 slice. The times are simulated.
32 devices in a mesh: dp: 1 (over z), ep: 32 (over y, x, core).
Axes of the slice: x: 4, y: 4, z: 1, core: 2. Of those that a mesh axis runs over, the one named last changes fastest.
The devices are a block of a 4x4x8 slice.
Arguments:
- x: bfloat16 [24576, 2048], P(('dp', 'ep'))
- route_idx: int32 [24576, 2], P(('dp', 'ep'))
- gates: float32 [24576, 2], P(('dp', 'ep'))
- w1: bfloat16 [32, 2048, 1408], P('ep')
- w3: bfloat16 [32, 2048, 1408], P('ep')
- w2: bfloat16 [32, 1408, 2048], P('ep')
Outputs:
- output: bfloat16 [24576, 2048], P(('dp', 'ep'))
All inputs are finite; a program needn't handle non-finite values.
Results may differ from a plain program's by a relative error of at most 0.00125.
Values are sent between devices in bfloat16 or wider.
A program may use at most 768 MiB of HBM per device.

v0:
```python
import jax
import jax.numpy as jnp
from jax import lax
from jax.sharding import PartitionSpec as P


def pair_slots(ne, e):
    n = e.shape[0]
    oh = (e[:, :, None] == jnp.arange(ne, dtype=e.dtype)).astype(jnp.float32)
    i = jnp.arange(n, dtype=jnp.int32)
    low = (i[None, :] < i[:, None]).astype(jnp.bfloat16)
    before = jnp.dot(low, jnp.sum(oh, axis=1).astype(jnp.bfloat16), preferred_element_type=jnp.float32)
    return jnp.sum(before[:, None, :] * oh, axis=2).astype(jnp.int32)


def dispatch(x, dest, nrows):
    r = jnp.arange(nrows, dtype=dest.dtype)[:, None]
    p = (dest[None, :, 0] == r) | (dest[None, :, 1] == r)
    return jnp.dot(p.astype(x.dtype), x)


def combine(back, dest, gates):
    r = jnp.arange(back.shape[0], dtype=dest.dtype)[None, :]
    o0 = jnp.dot((dest[:, 0:1] == r).astype(back.dtype), back, preferred_element_type=jnp.float32)
    o1 = jnp.dot((dest[:, 1:2] == r).astype(back.dtype), back, preferred_element_type=jnp.float32)
    return (gates[:, 0:1] * o0 + gates[:, 1:2] * o1).astype(jnp.bfloat16)


def expert_rows(rows, w1, w3, w2):
    a = jnp.dot(rows, w1, preferred_element_type=jnp.float32)
    b = jnp.dot(rows, w3, preferred_element_type=jnp.float32)
    h = (jax.nn.silu(a) * b).astype(jnp.bfloat16)
    return jnp.dot(h, w2, preferred_element_type=jnp.float32).astype(jnp.bfloat16)


def solution(mesh):
    ep = mesh.shape['ep']

    def local(x, route_idx, gates, w1, w3, w2):
        tok, d = x.shape
        cap = 3 * tok // 4
        dest = route_idx * cap + pair_slots(ep, route_idx)
        send = dispatch(x, dest, ep * cap).reshape(ep, cap, d)
        recv = lax.all_to_all(send, 'ep', 0, 0, tiled=True)
        out = lax.map(lambda rows: expert_rows(rows, w1[0], w3[0], w2[0]), recv)
        back = lax.all_to_all(out, 'ep', 0, 0, tiled=True)
        return combine(back.reshape(ep * cap, d), dest, gates)

    spec = P(('dp', 'ep'), None)
    wspec = P('ep', None, None)
    return jax.shard_map(local, mesh=mesh, in_specs=(spec, spec, spec, wspec, wspec, wspec),
                         out_specs=spec, check_vma=False)
```

profile of v0, /device:TPU:103, one launch (start us, length us, event | category | flops | bytes accessed | tf_op | source)
XLA Modules:
  0.0 2977.5 jit_solution(3576014001542526768)
XLA Ops:
  2.7 64.9 %fusion.35 = bf16[18432,2048]{1,0:T(8,128)(2,1)} fusion(bf16[768,2048]{1,0:T(8,128)(2,1)S(1)} %copy-done, s32[768]{0:T(1024)S(1)} %get-tuple-element.41, s32[768]{0:T(1024)S(1)} %get-tuple-element.40), kind=kOutput, calls=%fused_computation.24 | convolution fusion | flops 58024525824 | bytes 78649344 | tf_op jit(solution)/shard_map/dot_general | solution.py:19
  75.7 986.5 %all-to-all-done = bf16[32,576,2048]{2,1,0:T(8,128)(2,1)} async-done(((bf16[32,576,2048]{2,1,0:T(8,128)(2,1)}), bf16[32,576,2048]{2,1,0:T(8,128)(2,1)}, u32[]{:S(2)}, u32[]{:S(2)}) %all-to-all-start) | async-done | bytes 75497504 | tf_op jit(solution)/shard_map/all_to_all | solution.py:44
  1062.2 761.7 %while.10 = (s32[]{:T(128)}, bf16[32,576,2048]{2,1,0:T(8,128)(2,1)}, bf16[32,576,2048]{2,1,0:T(8,128)(2,1)}, bf16[1,2048,1408]{2,1,0:T(8,128)(2,1)}, bf16[1,2048...) while((s32[]{:T(128)}, bf16[32,576,2048]{2,1,0:T(8,128)(2,1)}, ...), condition=%wide.region_3.4_spmd, body=%wide.region_2.3_spmd.sunk | while | flops 9971712000 | bytes 30869068 | solution.py:45
  1071.1 15.0 fusion.68
  1094.9 15.0 fusion.68
  1118.7 15.0 fusion.68
  1142.5 14.9 fusion.68
  1166.3 15.0 fusion.68
  1190.2 15.0 fusion.68
  1214.0 14.9 fusion.68
  1237.8 15.0 fusion.68
  1261.6 15.0 fusion.68
  1285.4 15.0 fusion.68
  1309.3 14.9 fusion.68
  1356.8 14.9 fusion.68
  1380.6 14.9 fusion.68
  1404.4 14.9 fusion.68
  1452.0 15.0 fusion.68
  1499.6 14.9 fusion.68
  1523.4 14.9 fusion.68
  1570.9 14.9 fusion.68
  1618.5 15.0 fusion.68
  1666.1 14.9 fusion.68
  1689.9 14.9 fusion.68
  1713.7 15.0 fusion.68
  1737.5 15.0 fusion.68
  1785.1 15.0 fusion.68
  1809.0 14.9 fusion.68
  1823.9 33.1 %all-to-all-start.1 = ((bf16[32,576,2048]{2,1,0:T(8,128)(2,1)}), bf16[32,576,2048]{2,1,0:T(8,128)(2,1)}, u32[]{:S(2)}, u32[]{:S(2)}) async-start(bf16[32,576,2048]{2,1,0:T(8,128)(2,1)} %get-tuple-element.37), calls=%async_computation.1 | async-start | bytes 150994944 | tf_op jit(solution)/shard_map/all_to_all | solution.py:46
  1880.4 963.2 %all-to-all-done.1 = bf16[32,576,2048]{2,1,0:T(8,128)(2,1)} async-done(((bf16[32,576,2048]{2,1,0:T(8,128)(2,1)}), bf16[32,576,2048]{2,1,0:T(8,128)(2,1)}, u32[]{:S(2)}, u32[]{:S(2)}) %all-to-all-start.1) | async-done | bytes 75497504 | tf_op jit(solution)/shard_map/all_to_all | solution.py:46
  2843.6 66.3 %fusion.33 = f32[768,2048]{1,0:T(8,128)} fusion(bf16[18432,2048]{1,0:T(8,128)(2,1)} %bitcast.6, pred[768,18432]{1,0:T(32,128)(4,1)} %iota_compare_fusion.16), kind=kOutput, calls=%fused_computation.22 | convolution fusion | flops 57982058496 | bytes 95944704 | tf_op jit(solution)/shard_map/dot_general | solution.py:24
  2909.9 67.6 %add_convert_fusion = bf16[768,2048]{1,0:T(8,128)(2,1)} fusion(f32[768,2048]{1,0:T(8,128)} %fusion.33, bf16[18432,2048]{1,0:T(8,128)(2,1)} %bitcast.6, f32[768]{0:T(1024)S(1)} %get-tuple-element.39, f32[768]{0:T(1024)S(1)} %get-tuple-element.38, pred[768,18432]{1,0:T(32,128)(4,1)} %iota_compare_fusion.17), kind=kOutput, calls=%fused_computation.30 | convolution fusion | flops 57988349952 | bytes 99096576 | tf_op jit(solution)/shard_map/dot_general | solution.py:25
  (61 shorter events, 421.7 us)
Async XLA Ops:
  0.0 2.7 copy-start
  2.7 65.0 %copy-start.1 = (s32[768]{0:T(1024)}, s32[768]{0:T(1024)S(1)}, u32[]{:S(2)}) copy-start(s32[768]{0:T(1024)S(1)} %get-tuple-element.41) | copy-start | bytes 9220
  2.7 65.0 %copy-start.3 = (s32[768]{0:T(1024)}, s32[768]{0:T(1024)S(1)}, u32[]{:S(2)}) copy-start(s32[768]{0:T(1024)S(1)} %get-tuple-element.40) | copy-start | bytes 9220
  67.7 994.6 %all-to-all-start = ((bf16[32,576,2048]{2,1,0:T(8,128)(2,1)}), bf16[32,576,2048]{2,1,0:T(8,128)(2,1)}, u32[]{:S(2)}, u32[]{:S(2)}) async-start(bf16[32,576,2048]{2,1,0:T(8,128)(2,1)} %bitcast.5), calls=%async_computation | async-start | bytes 150994944 | tf_op jit(solution)/shard_map/all_to_all | solution.py:44
  1823.9 33.2 %copy-start.5 = (f32[768,2]{0,1:T(2,128)S(1)}, f32[768,2]{0,1:T(2,128)}, u32[]{:S(2)}) copy-start(f32[768,2]{0,1:T(2,128)} %param.10) | copy-start | bytes 18436
  1823.9 33.2 %copy-start.4 = (s32[768]{0:T(1024)S(1)}, s32[768]{0:T(1024)}, u32[]{:S(2)}) copy-start(s32[768]{0:T(1024)} %copy-done.3) | copy-start | bytes 9220
  1823.9 1019.7 %all-to-all-start.1 = ((bf16[32,576,2048]{2,1,0:T(8,128)(2,1)}), bf16[32,576,2048]{2,1,0:T(8,128)(2,1)}, u32[]{:S(2)}, u32[]{:S(2)}) async-start(bf16[32,576,2048]{2,1,0:T(8,128)(2,1)} %get-tuple-element.37), calls=%async_computation.1 | async-start | bytes 150994944 | tf_op jit(solution)/shard_map/all_to_all | solution.py:46
  1857.1 11.7 copy-start.2
where the time goes:
time: 3010 us; the launch traced here: 2980 us
  waiting for transfers between devices  1950 us (65%)
  matrix products  961 us (32%)
  starting transfers between devices  41.2 us (1%)
    all_to_all x1, waiting for transfers between devices, local(): recv = lax.all_to_all(send, 'ep', 0, 0, tiled=True)  987 us
    all_to_all x1, waiting for transfers between devices, local(): back = lax.all_to_all(out, 'ep', 0, 0, tiled=True)  963 us
    dot_general x32, matrix products, expert_rows(): jnp.dot(h, w2, preferred_element_type=jnp.float32).astype(jnp.bfloat16)  478 us
    dot_general x32, matrix products, expert_rows(): a = jnp.dot(rows, w1, preferred_element_type=jnp.float32)  283 us
    dot_general x1, matrix products, combine(): jnp.dot((dest[:, 1:2] == r).astype(back.dtype), back, preferred_element_t...  67.6 us
    dot_general x1, matrix products, combine(): jnp.dot((dest[:, 0:1] == r).astype(back.dtype), back, preferred_element_t...  66.3 us
    dot_general x1, matrix products, dispatch(): return jnp.dot(p.astype(x.dtype), x)  64.9 us
  transfers between devices with their start and end apart: 2, of which 2 were waited for; matrix products, arithmetic and copies ran while one was open for 1% of the time, Pallas kernels for 0%

commit v1 on v0

v1 whole, which is shorter than its diff:
```python
import jax
import jax.numpy as jnp
from jax import lax
from jax.sharding import PartitionSpec as P

CAP = 40
ROUND_COST = 200
HOT_COST = 100


def pair_slots(oh):
    n = oh.shape[0]
    i = jnp.arange(n, dtype=jnp.int32)
    low = (i[None, :] < i[:, None]).astype(jnp.bfloat16)
    before = jnp.dot(low, jnp.sum(oh, axis=1).astype(jnp.bfloat16), preferred_element_type=jnp.float32)
    return jnp.sum(before[:, None, :] * oh, axis=2).astype(jnp.int32)


def plan(most):
    ne = most.shape[0]
    i = jnp.arange(ne, dtype=jnp.int32)
    ahead = (most[None, :] > most[:, None]) | ((most[None, :] == most[:, None]) & (i[None, :] < i[:, None]))
    rank = jnp.sum(ahead.astype(jnp.int32), axis=1)
    k = jnp.arange(ne + 1, dtype=jnp.int32)
    left = jnp.max(jnp.where(rank[None, :] >= k[:, None], most[None, :], 0), axis=1)
    cost = k * HOT_COST + (left + CAP - 1) // CAP * ROUND_COST
    nhot = jnp.argmin(cost).astype(jnp.int32)
    rounds = jnp.sum(jnp.where(k == nhot, (left + CAP - 1) // CAP, 0))
    order = jnp.sum(jnp.where(rank[None, :] == i[:, None], i[None, :], 0), axis=1)
    return rank, order, nhot, rounds


def experts(rows, w1, w3, w2):
    a = jnp.dot(rows, w1, preferred_element_type=jnp.float32)
    b = jnp.dot(rows, w3, preferred_element_type=jnp.float32)
    h = (jax.nn.silu(a) * b).astype(jnp.bfloat16)
    return jnp.dot(h, w2, preferred_element_type=jnp.float32).astype(jnp.bfloat16)


def take(x, dest, nrows):
    r = jnp.arange(nrows, dtype=dest.dtype)[:, None]
    p = (dest[None, :, 0] == r) | (dest[None, :, 1] == r)
    return jnp.dot(p.astype(x.dtype), x)


def put(back, dest, gates):
    r = jnp.arange(back.shape[0], dtype=dest.dtype)[None, :]
    o0 = jnp.dot((dest[:, 0:1] == r).astype(back.dtype), back, preferred_element_type=jnp.float32)
    o1 = jnp.dot((dest[:, 1:2] == r).astype(back.dtype), back, preferred_element_type=jnp.float32)
    return gates[:, 0:1] * o0 + gates[:, 1:2] * o1


def solution(mesh):
    ep = mesh.shape['ep']

    def local(x, route_idx, gates, w1, w3, w2):
        tok, d = x.shape
        w1, w3, w2 = w1[0], w3[0], w2[0]
        me = lax.axis_index('ep')
        oh = (route_idx[:, :, None] == jnp.arange(ep, dtype=route_idx.dtype)).astype(jnp.float32)
        pos = pair_slots(oh)
        most = lax.pmax(jnp.sum(oh, axis=(0, 1)).astype(jnp.int32), 'ep')
        rank, order, nhot, rounds = plan(most)
        rk = jnp.sum(oh * rank.astype(jnp.float32), axis=2).astype(jnp.int32)
        cold = rk >= nhot

        def one_round(r, y):
            here = cold & (pos // CAP == r)
            dest = jnp.where(here, route_idx * CAP + pos - r * CAP, -1)
            send = take(x, dest, ep * CAP).reshape(ep, CAP, d)
            recv = lax.all_to_all(send, 'ep', 0, 0, tiled=True).reshape(ep * CAP, d)
            out = experts(recv, w1, w3, w2).reshape(ep, CAP, d)
            back = lax.all_to_all(out, 'ep', 0, 0, tiled=True).reshape(ep * CAP, d)
            return y + put(back, dest, gates)

        def one_hot(j, y):
            e = jnp.sum(jnp.where(jnp.arange(ep) == j, order, 0))
            mine = me == e
            v1, v3, v2 = lax.psum(tuple(jnp.where(mine, w, jnp.zeros_like(w)) for w in (w1, w3, w2)), 'ep')
            n = 3 * tok // 4
            dest = jnp.where(rk == j, pos, -1)
            out = experts(take(x, dest, n), v1, v3, v2)
            return y + put(out, dest, gates)

        y = jnp.zeros((tok, d), jnp.float32)
        y = lax.fori_loop(0, rounds, one_round, y)
        y = lax.fori_loop(0, nhot, one_hot, y)
        return y.astype(jnp.bfloat16)

    spec = P(('dp', 'ep'), None)
    wspec = P('ep', None, None)
    return jax.shard_map(local, mesh=mesh, in_specs=(spec, spec, spec, wspec, wspec, wspec),
                         out_specs=spec, check_vma=False)
```

time: 3010 us -> 485 us (0.16); the launches traced: 2980 us -> 484 us
  waiting for transfers between devices: 1950 us -> 138 us
  matrix products: 961 us -> 113 us
  blocking collectives: 0 us -> 184 us
    all_to_all x2, waiting for transfers between devices: 1950 us -> 138 us  [one_round(): back = lax.all_to_all(out, 'ep', 0, 0, tiled=True).reshape(ep * CAP, d)]
    dot_general x67 -> x10, matrix products: 960 us -> 113 us  [the longest x2 49.3 us: experts(): jnp.dot(h, w2, preferred_element_type=jnp.float32).astype(jnp.bfloat16)]
    all_to_all x0 -> x2, blocking collectives: none -> 137 us  [one_round(): recv = lax.all_to_all(send, 'ep', 0, 0, tiled=True).reshape(ep * CAP, d)]
    pmax x0 -> x1, blocking collectives: none -> 46.6 us  [local(): most = lax.pmax(jnp.sum(oh, axis=(0, 1)).astype(jnp.int32), 'ep')]
  transfers between devices with their start and end apart: 2 -> 2, of which waited for: 2 -> 2; matrix products, arithmetic and copies ran while one was open for 1% -> 0% of each run, Pallas kernels for 0% -> 0%
where the time goes in v1:
time: 485 us; the launch traced here: 484 us
  blocking collectives  184 us (38%)
  waiting for transfers between devices  138 us (28%)
  matrix products  113 us (23%)
  between operations  13.5 us (3%)
  starting transfers between devices  12.8 us (3%)
  other arithmetic  10.5 us (2%)
  local copies, waits for them, and re-layouts  8.9 us (2%)
    all_to_all x2, waiting for transfers between devices, one_round(): back = lax.all_to_all(out, 'ep', 0, 0, tiled=True).reshape(ep * CAP, d)  138 us
    all_to_all x2, blocking collectives, one_round(): recv = lax.all_to_all(send, 'ep', 0, 0, tiled=True).reshape(ep * CAP, d)  137 us
    dot_general x2, matrix products, experts(): jnp.dot(h, w2, preferred_element_type=jnp.float32).astype(jnp.bfloat16)  49.3 us
    pmax x1, blocking collectives, local(): most = lax.pmax(jnp.sum(oh, axis=(0, 1)).astype(jnp.int32), 'ep')  46.6 us
    dot_general x2, matrix products, experts(): a = jnp.dot(rows, w1, preferred_element_type=jnp.float32)  20.6 us
    dot_general x2, matrix products, put(): jnp.dot((dest[:, 1:2] == r).astype(back.dtype), back, preferred_element_t...  17.4 us
    all_to_all x2, starting transfers between devices, one_round(): back = lax.all_to_all(out, 'ep', 0, 0, tiled=True).reshape(ep * CAP, d)  12.8 us
    dot_general x2, matrix products, put(): jnp.dot((dest[:, 0:1] == r).astype(back.dtype), back, preferred_element_t...  12.8 us
  transfers between devices with their start and end apart: 2, of which 2 were waited for; matrix products, arithmetic and copies ran while one was open for 0% of the time, Pallas kernels for 0%

profile of v1, /device:TPU:103, one launch (start us, length us, event | category | flops | bytes accessed | tf_op | source)
XLA Modules:
  0.0 484.1 jit_solution(11266404035090713578)
XLA Ops:
  6.6 0.9 convert_reduce_fusion.1
  7.4 46.6 %pmax.7 = s32[32]{0:T(128)S(1)} all-reduce(s32[32]{0:T(128)S(1)} %convert_element_type.54), channel_id=1, replica_groups=mesh['dp'=1,'ep'=32] {'ep'}, use_global_device_ids=true, to_apply=%region_1.0 | all-reduce | flops 32 | bytes 256 | tf_op jit(solution)/shard_map/pmax | solution.py:62
  54.1 0.2 convert_reduce_fusion.2
  54.3 0.7 iota_reduce_fusion
  55.0 0.8 select_reduce_fusion
  55.9 0.6 broadcast_compare_fusion
  56.5 1.3 fusion.25
  57.8 0.3 fusion.21
  58.1 0.8 select_reduce_fusion.1
  58.9 3.4 broadcast_in_dim.36
  62.4 409.1 %while.22 = (s32[]{:T(128)}, f32[768,2048]{1,0:T(8,128)}, s32[]{:T(128)}, f32[768,2]{0,1:T(2,128)S(1)}, s32[768,2]{0,1:T(2,128)S(1)}, /*index=5*/s32[768,2]{0,1:...) while((s32[]{:T(128)}, f32[768,2048]{1,0:T(8,128)}, ...), condition=%wide.region_10.11_spmd, body=%wide.region_9.10_spmd.sunk | while | flops 34250182656 | bytes 200085344 | solution.py:86
  63.2 6.3 %fusion.90 = bf16[1280,2048]{1,0:T(8,128)(2,1)S(1)} fusion(bf16[768,2048]{1,0:T(8,128)(2,1)} %get-tuple-element.492, s32[768]{0:T(1024)S(1)} %get-tuple-element.431, s32[768]{0:T(1024)S(1)} %get-tuple-element.432), kind=kOutput, calls=%fused_computation.10.clone.1 | convolution fusion | flops 4029480960 | bytes 8394752 | tf_op jit(solution)/shard_map/while/body/dot_general | solution.py:43
  69.6 70.0 %all_to_all.18 = bf16[32,40,2048]{2,1,0:T(8,128)(2,1)S(1)} all-to-all(bf16[32,40,2048]{2,1,0:T(8,128)(2,1)S(1)} %bitcast.85), channel_id=1, replica_groups=mesh['dp'=1,'ep'=32] {'ep'}, dimensions={0} | all-to-all | bytes 10485760 | tf_op jit(solution)/shard_map/while/body/all_to_all | solution.py:71
  139.5 10.3 %fusion.91 = f32[1280,1408]{1,0:T(8,128)} fusion(bf16[1280,2048]{1,0:T(8,128)(2,1)S(1)} %bitcast.83, bf16[2048,1408]{1,0:T(8,128)(2,1)S(1)} %bitcast.80), kind=kOutput, calls=%fused_computation.70.clone.1 | convolution fusion | flops 7381975040 | bytes 18219008 | tf_op jit(solution)/shard_map/while/body/dot_general | solution.py:34
  149.8 24.6 %convolution_convert_fusion.4 = bf16[1280,2048]{1,0:T(8,128)(2,1)} fusion(bf16[1408,2048]{1,0:T(8,128)(2,1)} %get-tuple-element.495, bf16[1280,2048]{1,0:T(8,128)(2,1)} %bitcast.84, bf16[2048,1408]{1,0:T(8,128)(2,1)} %get-tuple-element.494, f32[1280,1408]{1,0:T(8,128)} %fusion.91), kind=kOutput, calls=%fused_computation.2.clone.1 | convolution fusion | flops 14777384960 | bytes 29229056 | tf_op jit(solution)/shard_map/while/body/dot_general | solution.py:37
  174.5 5.7 %all-to-all-start.1 = ((bf16[32,40,2048]{2,1,0:T(8,128)(2,1)}), bf16[32,40,2048]{2,1,0:T(8,128)(2,1)}, u32[]{:S(2)}, u32[]{:S(2)}) async-start(bf16[32,40,2048]{2,1,0:T(8,128)(2,1)} %bitcast.82), calls=%async_computation.1 | async-start | bytes 10485760 | tf_op jit(solution)/shard_map/while/body/all_to_all | solution.py:73
  180.2 69.2 %all-to-all-done.1 = bf16[32,40,2048]{2,1,0:T(8,128)(2,1)} async-done(((bf16[32,40,2048]{2,1,0:T(8,128)(2,1)}), bf16[32,40,2048]{2,1,0:T(8,128)(2,1)}, u32[]{:S(2)}, u32[]{:S(2)}) %all-to-all-start.1) | async-done | bytes 5242912 | tf_op jit(solution)/shard_map/while/body/all_to_all | solution.py:73
  249.4 6.4 %fusion.92 = f32[768,2048]{1,0:T(8,128)S(1)} fusion(bf16[1280,2048]{1,0:T(8,128)(2,1)} %bitcast.66, s32[768]{0:T(1024)S(1)} %get-tuple-element.432), kind=kOutput, calls=%fused_computation.8.clone.1 | convolution fusion | flops 4027514880 | bytes 11537408 | tf_op jit(solution)/shard_map/while/body/dot_general | solution.py:48
  255.9 8.7 %add_add_fusion.4 = f32[768,2048]{1,0:T(8,128)S(1)} fusion(f32[768,2048]{1,0:T(8,128)S(1)} %bitcast.76, f32[768,2048]{1,0:T(8,128)S(1)} %fusion.92, f32[768]{0:T(1024)S(1)} %get-tuple-element.433, f32[768]{0:T(1024)S(1)} %get-tuple-element.434, bf16[1280,2048]{1,0:T(8,128)(2,1)} %bitcast.66, s32[768]{0:T(1024)S(1)} %get-tuple-element.431), kind=kOutput, calls=%fused_computation.3.clone.1 | convolution fusion | flops 4033806336 | bytes 24126464 | tf_op jit(solution)/shard_map/while/body/dot_general | solution.py:49
  264.6 2.6 copy-done
  267.9 6.3 %fusion.90 = bf16[1280,2048]{1,0:T(8,128)(2,1)S(1)} fusion(bf16[768,2048]{1,0:T(8,128)(2,1)} %get-tuple-element.492, s32[768]{0:T(1024)S(1)} %get-tuple-element.431, s32[768]{0:T(1024)S(1)} %get-tuple-element.432), kind=kOutput, calls=%fused_computation.10.clone.1 | convolution fusion | flops 4029480960 | bytes 8394752 | tf_op jit(solution)/shard_map/while/body/dot_general | solution.py:43
  274.2 67.4 %all_to_all.18 = bf16[32,40,2048]{2,1,0:T(8,128)(2,1)S(1)} all-to-all(bf16[32,40,2048]{2,1,0:T(8,128)(2,1)S(1)} %bitcast.85), channel_id=1, replica_groups=mesh['dp'=1,'ep'=32] {'ep'}, dimensions={0} | all-to-all | bytes 10485760 | tf_op jit(solution)/shard_map/while/body/all_to_all | solution.py:71
  341.6 10.3 %fusion.91 = f32[1280,1408]{1,0:T(8,128)} fusion(bf16[1280,2048]{1,0:T(8,128)(2,1)S(1)} %bitcast.83, bf16[2048,1408]{1,0:T(8,128)(2,1)S(1)} %bitcast.80), kind=kOutput, calls=%fused_computation.70.clone.1 | convolution fusion | flops 7381975040 | bytes 18219008 | tf_op jit(solution)/shard_map/while/body/dot_general | solution.py:34
  351.9 24.6 %convolution_convert_fusion.4 = bf16[1280,2048]{1,0:T(8,128)(2,1)} fusion(bf16[1408,2048]{1,0:T(8,128)(2,1)} %get-tuple-element.495, bf16[1280,2048]{1,0:T(8,128)(2,1)} %bitcast.84, bf16[2048,1408]{1,0:T(8,128)(2,1)} %get-tuple-element.494, f32[1280,1408]{1,0:T(8,128)} %fusion.91), kind=kOutput, calls=%fused_computation.2.clone.1 | convolution fusion | flops 14777384960 | bytes 29229056 | tf_op jit(solution)/shard_map/while/body/dot_general | solution.py:37
  376.6 7.1 %all-to-all-start.1 = ((bf16[32,40,2048]{2,1,0:T(8,128)(2,1)}), bf16[32,40,2048]{2,1,0:T(8,128)(2,1)}, u32[]{:S(2)}, u32[]{:S(2)}) async-start(bf16[32,40,2048]{2,1,0:T(8,128)(2,1)} %bitcast.82), calls=%async_computation.1 | async-start | bytes 10485760 | tf_op jit(solution)/shard_map/while/body/all_to_all | solution.py:73
  383.7 69.2 %all-to-all-done.1 = bf16[32,40,2048]{2,1,0:T(8,128)(2,1)} async-done(((bf16[32,40,2048]{2,1,0:T(8,128)(2,1)}), bf16[32,40,2048]{2,1,0:T(8,128)(2,1)}, u32[]{:S(2)}, u32[]{:S(2)}) %all-to-all-start.1) | async-done | bytes 5242912 | tf_op jit(solution)/shard_map/while/body/all_to_all | solution.py:73
  452.9 6.4 %fusion.92 = f32[768,2048]{1,0:T(8,128)S(1)} fusion(bf16[1280,2048]{1,0:T(8,128)(2,1)} %bitcast.66, s32[768]{0:T(1024)S(1)} %get-tuple-element.432), kind=kOutput, calls=%fused_computation.8.clone.1 | convolution fusion | flops 4027514880 | bytes 11537408 | tf_op jit(solution)/shard_map/while/body/dot_general | solution.py:48
  459.3 8.7 %add_add_fusion.4 = f32[768,2048]{1,0:T(8,128)S(1)} fusion(f32[768,2048]{1,0:T(8,128)S(1)} %bitcast.76, f32[768,2048]{1,0:T(8,128)S(1)} %fusion.92, f32[768]{0:T(1024)S(1)} %get-tuple-element.433, f32[768]{0:T(1024)S(1)} %get-tuple-element.434, bf16[1280,2048]{1,0:T(8,128)(2,1)} %bitcast.66, s32[768]{0:T(1024)S(1)} %get-tuple-element.431), kind=kOutput, calls=%fused_computation.3.clone.1 | convolution fusion | flops 4033806336 | bytes 24126464 | tf_op jit(solution)/shard_map/while/body/dot_general | solution.py:49
  468.1 2.6 copy-done
  471.5 0.1 select_reduce_fusion.2
  471.7 0.6 while.23
  472.3 4.9 %convert_element_type.60 = bf16[768,2048]{1,0:T(8,128)(2,1)} convert(f32[768,2048]{1,0:T(8,128)} %get-tuple-element.218) | non-fusion elementwise | flops 1572864 | bytes 9437184 | tf_op jit(solution)/shard_map/convert_element_type | solution.py:88
  (50 shorter events, 0.4 us)
Async XLA Ops:
  6.5 55.8 %copy-start.3 = (s32[768,2]{0,1:T(2,128)S(1)}, s32[768,2]{0,1:T(2,128)}, u32[]{:S(2)}) copy-start(s32[768,2]{0,1:T(2,128)} %param.11) | copy-start | bytes 18436
  6.5 55.8 %copy-start.2 = (f32[768,2]{0,1:T(2,128)S(1)}, f32[768,2]{0,1:T(2,128)}, u32[]{:S(2)}) copy-start(f32[768,2]{0,1:T(2,128)} %param.12) | copy-start | bytes 18436
  54.3 0.8 copy-start.6
  55.8 3.0 copy-start.4
  62.4 409.2 %copy-start.5 = (f32[768,2]{0,1:T(2,128)S(1)}, f32[768,2]{0,1:T(2,128)}, u32[]{:S(2)}) copy-start(f32[768,2]{0,1:T(2,128)} %copy-done.4) | copy-start | bytes 18436
  62.4 409.2 %copy-start.7 = (s32[32]{0:T(128)S(1)}, s32[32]{0:T(128)}, u32[]{:S(2)}) copy-start(s32[32]{0:T(128)} %copy-done.6) | copy-start | bytes 388
  69.6 70.0 %slice-start.2 = ((s8[5767168]{0:T(1024)(128)(4,1)}), s8[4194304]{0:T(1024)(128)(4,1)S(1)}, s32[]{:S(2)}) async-start(s8[5767168]{0:T(1024)(128)(4,1)} %bitcast.79), calls=%async_computation.5 | async-start | bytes 8388608 | tf_op jit(solution)/shard_map/while
  69.6 70.0 %slice-start.3 = ((s8[5767168]{0:T(1024)(128)(4,1)}), s8[1572864]{0:T(1024)(128)(4,1)S(1)}, s32[]{:S(2)}) async-start(s8[5767168]{0:T(1024)(128)(4,1)} %bitcast.79), calls=%async_computation.6 | async-start | bytes 3145728 | tf_op jit(solution)/shard_map/while
  139.5 10.3 %copy-start.1 = (bf16[32,40,2048]{2,1,0:T(8,128)(2,1)}, bf16[32,40,2048]{2,1,0:T(8,128)(2,1)S(1)}, u32[]{:S(2)}) copy-start(bf16[32,40,2048]{2,1,0:T(8,128)(2,1)S(1)} %all_to_all.18) | copy-start | bytes 15728644 | tf_op jit(solution)/shard_map/while
  174.5 81.3 %slice-start = ((s8[6291456]{0:T(1024)(128)(4,1)}), s8[2097152]{0:T(1024)(128)(4,1)S(1)}, s32[]{:S(2)}) async-start(s8[6291456]{0:T(1024)(128)(4,1)} %bitcast.75), calls=%async_computation.3 | async-start | bytes 4194304 | tf_op jit(solution)/shard_map/while
  174.5 74.9 %all-to-all-start.1 = ((bf16[32,40,2048]{2,1,0:T(8,128)(2,1)}), bf16[32,40,2048]{2,1,0:T(8,128)(2,1)}, u32[]{:S(2)}, u32[]{:S(2)}) async-start(bf16[32,40,2048]{2,1,0:T(8,128)(2,1)} %bitcast.82), calls=%async_computation.1 | async-start | bytes 10485760 | tf_op jit(solution)/shard_map/while/body/all_to_all | solution.py:73
  249.4 6.4 %slice-start.1 = ((s8[6291456]{0:T(1024)(128)(4,1)}), s8[4194304]{0:T(1024)(128)(4,1)S(1)}, s32[]{:S(2)}) async-start(s8[6291456]{0:T(1024)(128)(4,1)} %bitcast.75), calls=%async_computation.4 | async-start | bytes 8388608 | tf_op jit(solution)/shard_map/while
  264.6 2.7 copy-start
  274.2 67.4 %slice-start.2 = ((s8[5767168]{0:T(1024)(128)(4,1)}), s8[4194304]{0:T(1024)(128)(4,1)S(1)}, s32[]{:S(2)}) async-start(s8[5767168]{0:T(1024)(128)(4,1)} %bitcast.79), calls=%async_computation.5 | async-start | bytes 8388608 | tf_op jit(solution)/shard_map/while
  274.2 67.4 %slice-start.3 = ((s8[5767168]{0:T(1024)(128)(4,1)}), s8[1572864]{0:T(1024)(128)(4,1)S(1)}, s32[]{:S(2)}) async-start(s8[5767168]{0:T(1024)(128)(4,1)} %bitcast.79), calls=%async_computation.6 | async-start | bytes 3145728 | tf_op jit(solution)/shard_map/while
  341.6 10.3 %copy-start.1 = (bf16[32,40,2048]{2,1,0:T(8,128)(2,1)}, bf16[32,40,2048]{2,1,0:T(8,128)(2,1)S(1)}, u32[]{:S(2)}) copy-start(bf16[32,40,2048]{2,1,0:T(8,128)(2,1)S(1)} %all_to_all.18) | copy-start | bytes 15728644 | tf_op jit(solution)/shard_map/while
  376.6 82.8 %slice-start = ((s8[6291456]{0:T(1024)(128)(4,1)}), s8[2097152]{0:T(1024)(128)(4,1)S(1)}, s32[]{:S(2)}) async-start(s8[6291456]{0:T(1024)(128)(4,1)} %bitcast.75), calls=%async_computation.3 | async-start | bytes 4194304 | tf_op jit(solution)/shard_map/while
  376.6 76.3 %all-to-all-start.1 = ((bf16[32,40,2048]{2,1,0:T(8,128)(2,1)}), bf16[32,40,2048]{2,1,0:T(8,128)(2,1)}, u32[]{:S(2)}, u32[]{:S(2)}) async-start(bf16[32,40,2048]{2,1,0:T(8,128)(2,1)} %bitcast.82), calls=%async_computation.1 | async-start | bytes 10485760 | tf_op jit(solution)/shard_map/while/body/all_to_all | solution.py:73
  452.9 6.4 %slice-start.1 = ((s8[6291456]{0:T(1024)(128)(4,1)}), s8[4194304]{0:T(1024)(128)(4,1)S(1)}, s32[]{:S(2)}) async-start(s8[6291456]{0:T(1024)(128)(4,1)} %bitcast.75), calls=%async_computation.4 | async-start | bytes 8388608 | tf_op jit(solution)/shard_map/while
  468.1 2.7 copy-start

commit v2 on v1

--- a/solution.py
+++ b/solution.py
@@ -1,11 +1,311 @@
+import functools
+import math
+
 import jax
 import jax.numpy as jnp
 from jax import lax
+from jax.experimental import pallas as pl
+from jax.experimental.pallas import tpu as pltpu
 from jax.sharding import PartitionSpec as P
 
+MESH = pl.DeviceIdType.MESH
 CAP = 40
-ROUND_COST = 200
-HOT_COST = 100
+SLOTS = 3
+ROWS = 16
+LAG = 4
+TM = 192
+
+
+@functools.lru_cache(None)
+def rings(n):
+    def near(v):
+        y, x = divmod(v, n)
+        return [y * n + (x + 1) % n, y * n + (x - 1) % n, (y + 1) % n * n + x, (y - 1) % n * n + x]
+
+    def edges(c):
+        return {frozenset((c[i], c[(i + 1) % len(c)])) for i in range(len(c))}
+
+    def cycle(used):
+        v, c = 0, [0]
+        prev = None
+        while True:
+            step = [w for w in near(v) if frozenset((v, w)) not in used and w != prev]
+            prev, v = v, step[0]
+            if v == 0 or v in c:
+                return c
+            c.append(v)
+
+    def search(path, seen):
+        if len(path) == n * n:
+            if path[0] in near(path[-1]):
+                other = cycle(edges(path))
+                if len(other) == n * n and not edges(other) & edges(path):
+                    return list(path), other
+            return None
+        for w in near(path[-1]):
+            if w not in seen:
+                found = search(path + [w], seen | {w})
+                if found:
+                    return found
+        return None
+
+    a, b = search([0], {0})
+    nxt, pos = [], []
+    for c in (a, a[::-1], b, b[::-1]):
+        nx, ps = [0] * len(c), [0] * len(c)
+        for i, v in enumerate(c):
+            nx[v], ps[v] = c[(i + 1) % len(c)], i
+        nxt.append(nx)
+        pos.append(ps)
+    return nxt, pos
+
+
+def counts_kernel(ep, c_ref, out_ref, send_sem, recv_sem):
+    me = lax.axis_index('ep')
+    out_ref[me] = c_ref[...]
+
+    def send(i, _):
+        pltpu.make_async_remote_copy(
+            src_ref=c_ref, dst_ref=out_ref.at[me], send_sem=send_sem, recv_sem=recv_sem,
+            device_id={'ep': lax.rem(me + i, ep)}, device_id_type=MESH).start()
+        return 0
+
+    lax.fori_loop(1, ep, send, 0)
+    others = out_ref.at[pl.ds(0, ep - 1)]
+    pltpu.make_async_copy(others, others, send_sem).wait()
+    pltpu.make_async_copy(others, others, recv_sem).wait()
+
+
+def gather_counts(c, ep):
+    return pl.pallas_call(
+        functools.partial(counts_kernel, ep),
+        name='gather_counts',
+        out_shape=jax.ShapeDtypeStruct((ep,) + c.shape, c.dtype),
+        in_specs=[pl.BlockSpec(memory_space=pltpu.VMEM)],
+        out_specs=pl.BlockSpec(memory_space=pltpu.VMEM),
+        scratch_shapes=[pltpu.SemaphoreType.DMA, pltpu.SemaphoreType.DMA],
+        compiler_params=pltpu.CompilerParams(has_side_effects=True),
+    )(c)
+
+
+def ring_kernel(nxt, steps, mask_ref, w1_ref, w3_ref, w2_ref, out_ref, sib_ref, recv, inj,
+                s_next, s_sib, s_out, r_next, r_sib, sib_send, sib_recv, inj_sem):
+    chips = len(nxt[0])
+    own = (w1_ref, w3_ref, w2_ref)
+    per = w1_ref.shape[2]
+    chunks = len(own) * per
+    me = lax.axis_index('ep')
+    chip, core = me // 2, me % 2
+    sib = me + 1 - 2 * core
+    to = []
+    for r in range(4):
+        t = jnp.int32(0)
+        for i in range(chips):
+            t = jnp.where(chip == i, nxt[r][i], t)
+        to.append(t * 2 + core)
+    chains = [(j, r) for j in range(SLOTS) for r in range(4)]
+
+    def push(q):
+        return pltpu.make_async_remote_copy(
+            src_ref=own[q].at[1 - core], dst_ref=sib_ref.at[q], send_sem=sib_send.at[q],
+            recv_sem=sib_recv.at[q], device_id={'ep': sib}, device_id_type=MESH)
+
+    for q in range(len(own)):
+        push(q).start()
+
+    def loads(q, t):
+        k = lax.rem(t, LAG)
+        return (pltpu.make_async_copy(own[q].at[core, :, lax.rem(t, per)], inj.at[k, 0], inj_sem.at[k, 0]),
+                pltpu.make_async_copy(sib_ref.at[q, :, lax.rem(t, per)], inj.at[k, 1], inj_sem.at[k, 1]))
+
+    def fetch(t):
+        for q in range(len(own)):
+            @pl.when(t == q * per)
+            def _():
+                push(q).wait_recv()
+
+            @pl.when(t // per == q)
+            def _():
+                for c in loads(q, t):
+                    c.start()
+
+    def hop(t, j, r):
+        pltpu.make_async_remote_copy(
+            src_ref=recv.at[t, j, r], dst_ref=recv.at[t + 1, j, r], send_sem=s_next.at[lax.rem(t, LAG)],
+            recv_sem=r_next.at[lax.rem(t + 1, chips), j, r], device_id={'ep': to[r]}, device_id_type=MESH).start()
+
+    def keep(t):
+        pltpu.make_async_remote_copy(
+            src_ref=recv.at[t], dst_ref=out_ref.at[core, t], send_sem=s_sib.at[lax.rem(t, LAG)],
+            recv_sem=r_sib.at[t], device_id={'ep': sib}, device_id_type=MESH).start()
+        pltpu.make_async_copy(recv.at[t], out_ref.at[core, t], s_out.at[lax.rem(t, LAG)]).start()
+
+    def drain(t, last):
+        whole = recv.at[t]
+        for s in (s_sib, s_out) if last else (s_next, s_sib, s_out):
+            pltpu.make_async_copy(whole, whole, s.at[lax.rem(t, LAG)]).wait()
+
+    def arrive(t, j, r):
+        here = recv.at[t, j, r]
+        pltpu.make_async_copy(here, here, r_next.at[lax.rem(t, chips), j, r]).wait()
+
+    def step(t, first, inject, last):
+        if inject:
+            for c in loads(0, t):
+                c.wait()
+            k = lax.rem(t, LAG)
+
+            @pl.when(t + LAG - 1 < chunks)
+            def _():
+                fetch(t + LAG - 1)
+
+        @pl.when(t >= LAG - 1)
+        def _():
+            drain(t - (LAG - 1), False)
+
+        before = None
+        for j, r in chains:
+            if not first:
+                arrive(t, j, r)
+            if inject:
+                mine, theirs = mask_ref[j, 0] > 0, mask_ref[j, 1] > 0
+                for c in range(recv.shape[-1] // 128):
+                    cols = pl.ds(c * 128, 128)
+                    other = inj[k, 1, r, :, cols]
+                    old = other if first else recv[t, j, r, :, cols]
+                    recv[t, j, r, :, cols] = jnp.where(mine, inj[k, 0, r, :, cols], jnp.where(theirs, other, old))
+            if before is not None and not last:
+                hop(t, *before)
+            before = (j, r)
+        if not last:
+            hop(t, *before)
+        keep(t)
+
+    for t in range(LAG - 1):
+        fetch(jnp.int32(t))
+    step(jnp.int32(0), True, True, False)
+    lax.fori_loop(1, chunks, lambda t, c: (step(t, False, True, False), c)[1], 0)
+    lax.fori_loop(chunks, steps - 1, lambda t, c: (step(t, False, False, False), c)[1], 0)
+    step(jnp.int32(steps - 1), False, False, True)
+    for t in range(steps - LAG + 1, steps):
+        drain(jnp.int32(t), t == steps - 1)
+
+    def settle(t, c):
+        part = out_ref.at[1 - core, t]
+        pltpu.make_async_copy(part, part, r_sib.at[t]).wait()
+        return c
+
+    lax.fori_loop(0, steps, settle, 0)
+    for q in range(len(own)):
+        push(q).wait_send()
+
+
+def broadcast(masks, w1, w3, w2t, nxt):
+    _, nr, per, rows, cols = w1.shape
+    steps = 3 * per + len(nxt[0]) - 1
+    dma = pltpu.SemaphoreType.DMA
+    hbm = pl.BlockSpec(memory_space=pl.ANY)
+    out, _ = pl.pallas_call(
+        functools.partial(ring_kernel, nxt, steps),
+        name='ring_broadcast',
+        out_shape=(jax.ShapeDtypeStruct((2, steps, SLOTS, nr, rows, cols), w1.dtype),
+                   jax.ShapeDtypeStruct((3, nr, per, rows, cols), w1.dtype)),
+        in_specs=[pl.BlockSpec(memory_space=pltpu.VMEM), hbm, hbm, hbm],
+        out_specs=(hbm, hbm),
+        scratch_shapes=[
+            pltpu.VMEM((steps, SLOTS, nr, rows, cols), w1.dtype),
+            pltpu.VMEM((LAG, 2, nr, rows, cols), w1.dtype),
+            dma((LAG,)), dma((LAG,)), dma((LAG,)), dma((len(nxt[0]), SLOTS, nr)), dma((steps,)),
+            dma((3,)), dma((3,)), dma((LAG, 2)),
+        ],
+        compiler_params=pltpu.CompilerParams(has_side_effects=True, vmem_limit_bytes=60 * 1024 * 1024),
+    )(masks, w1, w3, w2t)
+    return out
+
+
+def hot_kernel(info_ref, x_ref, drow_ref, dcol_ref, gcol_ref, got_ref, y0_ref, y_ref,
+               w, a, b, h, xg, p2, w_sem, y_sem):
+    tok, d = x_ref.shape
+    nr = got_ref.shape[3]
+    per = w.shape[3]
+    f = got_ref.shape[5]
+    blk = per * ROWS
+
+    def loads(j, start):
+        for q in range(3):
+            for c in range(2):
+                for r in range(nr):
+                    cp = pltpu.make_async_copy(
+                        got_ref.at[c, pl.ds(info_ref[j, 1 + r] + q * per, per), j, r],
+                        w.at[j % 2, q, c * nr + r], w_sem.at[j % 2, q, c * nr + r])
+                    cp.start() if start else cp.wait()
+
+    loads(0, True)
+    fill = pltpu.make_async_copy(y0_ref, y_ref, y_sem)
+    fill.start()
+    fill.wait()
+    for j in range(SLOTS):
+        if j + 1 < SLOTS:
+            loads(j + 1, True)
+        loads(j, False)
+
+        def tile(m, carry, j=j):
+            base = m * TM
+            p = (drow_ref[j:j + 1, :] == base + lax.broadcasted_iota(jnp.int32, (TM, tok), 0)).astype(jnp.bfloat16)
+            p2[...] = (dcol_ref[:, j:j + 1] == base + lax.broadcasted_iota(jnp.int32, (tok, TM), 1)).astype(jnp.bfloat16)
+
+            def up(i, c):
+                cols = pl.ds(pl.multiple_of(i * blk, blk), blk)
+                xs = jnp.dot(p, x_ref[:, cols], preferred_element_type=jnp.float32).astype(jnp.bfloat16)
+                da = jnp.dot(xs, w[j % 2, 0, i].reshape(blk, f), preferred_element_type=jnp.float32)
+                db = jnp.dot(xs, w[j % 2, 1, i].reshape(blk, f), preferred_element_type=jnp.float32)
+
+                @pl.when(i == 0)
+                def _():
+                    a[...] = da
+                    b[...] = db
+
+                @pl.when(i > 0)
+                def _():
+                    a[...] += da
+                    b[...] += db
+                return c
+
+            lax.fori_loop(0, 2 * nr, up, 0)
+            h[...] = (jax.nn.silu(a[...]) * b[...]).astype(jnp.bfloat16)
+
+            def down(i, c):
+                cols = pl.ds(pl.multiple_of(i * blk, blk), blk)
+                o = lax.dot_general(h[...], w[j % 2, 2, i].reshape(blk, f), (((1,), (1,)), ((), ())),
+                                    preferred_element_type=jnp.float32).astype(jnp.bfloat16)
+                y_ref[:, cols] += gcol_ref[:, j:j + 1] * jnp.dot(p2[...], o, preferred_element_type=jnp.float32)
+                return c
+
+            lax.fori_loop(0, 2 * nr, down, 0)
+            return carry
+
+        lax.fori_loop(0, (info_ref[j, 0] + TM - 1) // TM, tile, 0)
+
+
+def hot_rows(info, x, drow, dcol, gcol, got, y0):
+    tok, d = x.shape
+    _, _, _, nr, rows, f = got.shape
+    per = d // (2 * nr * rows)
+    vmem, hbm = pl.BlockSpec(memory_space=pltpu.VMEM), pl.BlockSpec(memory_space=pl.ANY)
+    return pl.pallas_call(
+        hot_kernel,
+        name='hot_rows',
+        out_shape=jax.ShapeDtypeStruct(y0.shape, y0.dtype),
+        in_specs=[pl.BlockSpec(memory_space=pltpu.SMEM), vmem, vmem, vmem, vmem, hbm, hbm],
+        out_specs=vmem,
+        scratch_shapes=[
+            pltpu.VMEM((2, 3, 2 * nr, per, rows, f), x.dtype),
+            pltpu.VMEM((TM, f), jnp.float32), pltpu.VMEM((TM, f), jnp.float32), pltpu.VMEM((TM, f), x.dtype),
+            pltpu.VMEM((8, 128), x.dtype), pltpu.VMEM((tok, TM), x.dtype),
+            pltpu.SemaphoreType.DMA((2, 3, 2 * nr)), pltpu.SemaphoreType.DMA,
+        ],
+        compiler_params=pltpu.CompilerParams(vmem_limit_bytes=60 * 1024 * 1024),
+    )(info, x, drow, dcol, gcol, got, y0)
 
 
 def pair_slots(oh):
@@ -16,14 +316,15 @@
     return jnp.sum(before[:, None, :] * oh, axis=2).astype(jnp.int32)
 
 
-def plan(most):
+def plan(most, worst):
     ne = most.shape[0]
     i = jnp.arange(ne, dtype=jnp.int32)
     ahead = (most[None, :] > most[:, None]) | ((most[None, :] == most[:, None]) & (i[None, :] < i[:, None]))
     rank = jnp.sum(ahead.astype(jnp.int32), axis=1)
     k = jnp.arange(ne + 1, dtype=jnp.int32)
-    left = jnp.max(jnp.where(rank[None, :] >= k[:, None], most[None, :], 0), axis=1)
-    cost = k * HOT_COST + (left + CAP - 1) // CAP * ROUND_COST
+    left = worst(jnp.max(jnp.where(rank[None, :] >= k[:, None], most[None, :], 0), axis=1))
+    hot_cost = (k + SLOTS - 1) // SLOTS * 260 + k
+    cost = hot_cost + (left + CAP - 1) // CAP * 170
     nhot = jnp.argmin(cost).astype(jnp.int32)
     rounds = jnp.sum(jnp.where(k == nhot, (left + CAP - 1) // CAP, 0))
     order = jnp.sum(jnp.where(rank[None, :] == i[:, None], i[None, :], 0), axis=1)
@@ -52,15 +353,23 @@
 
 def solution(mesh):
     ep = mesh.shape['ep']
+    groups = mesh.shape['dp']
+    nxt, pos_of = rings(math.isqrt(ep // 2))
 
     def local(x, route_idx, gates, w1, w3, w2):
         tok, d = x.shape
         w1, w3, w2 = w1[0], w3[0], w2[0]
+        f = w1.shape[1]
+        w2t = w2.T
         me = lax.axis_index('ep')
-        oh = (route_idx[:, :, None] == jnp.arange(ep, dtype=route_idx.dtype)).astype(jnp.float32)
+        i = jnp.arange(ep, dtype=jnp.int32)
+        oh = (route_idx[:, :, None] == i).astype(jnp.float32)
         pos = pair_slots(oh)
-        most = lax.pmax(jnp.sum(oh, axis=(0, 1)).astype(jnp.int32), 'ep')
-        rank, order, nhot, rounds = plan(most)
+        mine = jnp.sum(oh, axis=(0, 1))
+        table = gather_counts(jnp.zeros((8, 128), jnp.float32).at[0, :ep].set(mine), ep)
+        most = jnp.max(table[:, 0, :ep], axis=0).astype(jnp.int32)
+        worst = (lambda v: lax.pmax(v, 'dp')) if groups > 1 else (lambda v: v)
+        rank, order, nhot, rounds = plan(most, worst)
         rk = jnp.sum(oh * rank.astype(jnp.float32), axis=2).astype(jnp.int32)
         cold = rk >= nhot
 
@@ -73,18 +382,28 @@
             back = lax.all_to_all(out, 'ep', 0, 0, tiled=True).reshape(ep * CAP, d)
             return y + put(back, dest, gates)
 
-        def one_hot(j, y):
-            e = jnp.sum(jnp.where(jnp.arange(ep) == j, order, 0))
-            mine = me == e
-            v1, v3, v2 = lax.psum(tuple(jnp.where(mine, w, jnp.zeros_like(w)) for w in (w1, w3, w2)), 'ep')
-            n = 3 * tok // 4
-            dest = jnp.where(rk == j, pos, -1)
-            out = experts(take(x, dest, n), v1, v3, v2)
-            return y + put(out, dest, gates)
+        def some_hot(it, y):
+            shape = (2, 4, -1, ROWS, f)
+            slot = it * SLOTS + jnp.arange(SLOTS, dtype=jnp.int32)
+            src = jnp.sum(jnp.where(i[None, :] == slot[:, None], order[None, :], 0), axis=1)
+            flags = jnp.stack([src == me, src == me + 1 - 2 * (me % 2)], axis=1)
+            masks = jnp.broadcast_to(flags[:, :, None, None], (SLOTS, 2, ROWS, 128)).astype(jnp.bfloat16)
+            got = broadcast(masks, w1.reshape(shape), w3.reshape(shape), w2t.reshape(shape), nxt)
+            place = jnp.array(pos_of, jnp.int32)
+            chip = jnp.arange(ep // 2, dtype=jnp.int32)
+            at = jnp.sum(jnp.where(chip == me // 2, place, 0), axis=1)[None, :]
+            at = at - jnp.sum(jnp.where((chip[None, :] == src[:, None] // 2)[:, None, :], place[None], 0), axis=2)
+            at = jnp.where(at < 0, at + ep // 2, at)
+            match = (rk[:, :, None] == slot) & (rk < nhot)[:, :, None]
+            dcol = jnp.sum(jnp.where(match, pos[:, :, None] + 1, 0), axis=1) - 1
+            gcol = jnp.sum(jnp.where(match, gates[:, :, None], 0), axis=1)
+            cnt = jnp.sum((dcol >= 0).astype(jnp.int32), axis=0)
+            info = jnp.concatenate([cnt[:, None], at], axis=1)
+            return hot_rows(info, x, dcol.T, dcol, gcol, got, y)
 
         y = jnp.zeros((tok, d), jnp.float32)
         y = lax.fori_loop(0, rounds, one_round, y)
-        y = lax.fori_loop(0, nhot, one_hot, y)
+        y = lax.fori_loop(0, (nhot + SLOTS - 1) // SLOTS, some_hot, y)
         return y.astype(jnp.bfloat16)
 
     spec = P(('dp', 'ep'), None)

time: 485 us -> 454 us (0.936)
  blocking collectives: 184 us -> 138 us
  Pallas kernels: 0 us -> 15 us
  between operations: 13.5 us -> 0.82 us
  local copies, waits for them, and re-layouts: 8.9 us -> 18.1 us
    pmax x1 -> x0, blocking collectives: 46.6 us -> none  [local(): most = lax.pmax(jnp.sum(oh, axis=(0, 1)).astype(jnp.int32), 'ep')]
    pallas_call x0 -> x1, Pallas kernels: none -> 15 us  [gather_counts(): pl.pallas_call(functools.partial(counts_kernel, ep), name='gather_counts'...]
    unnamed x12 -> x13, local copies, waits for them, and re-layouts: 0.02 us -> 8.4 us
where the time goes in v2:
time: 454 us; the launch traced here: 453 us
  blocking collectives  138 us (30%)
  waiting for transfers between devices  138 us (30%)
  matrix products  113 us (25%)
  local copies, waits for them, and re-layouts  18.1 us (4%)
  starting transfers between devices  15.7 us (3%)
  Pallas kernels  15 us (3%)
  other arithmetic  12.2 us (3%)
    all_to_all x2, waiting for transfers between devices, one_round(): back = lax.all_to_all(out, 'ep', 0, 0, tiled=True).reshape(ep * CAP, d)  138 us
    all_to_all x2, blocking collectives, one_round(): recv = lax.all_to_all(send, 'ep', 0, 0, tiled=True).reshape(ep * CAP, d)  138 us
    dot_general x2, matrix products, experts(): jnp.dot(h, w2, preferred_element_type=jnp.float32).astype(jnp.bfloat16)  49.1 us
    dot_general x2, matrix products, experts(): a = jnp.dot(rows, w1, preferred_element_type=jnp.float32)  20.7 us
    dot_general x2, matrix products, put(): jnp.dot((dest[:, 1:2] == r).astype(back.dtype), back, preferred_element_t...  17.4 us
    all_to_all x2, starting transfers between devices, one_round(): back = lax.all_to_all(out, 'ep', 0, 0, tiled=True).reshape(ep * CAP, d)  15.7 us
    pallas_call x1, Pallas kernels, gather_counts(): pl.pallas_call(functools.partial(counts_kernel, ep), name='gather_counts'...  15 us
    dot_general x2, matrix products, put(): jnp.dot((dest[:, 0:1] == r).astype(back.dtype), back, preferred_element_t...  12.8 us
  transfers between devices with their start and end apart: 2, of which 2 were waited for; matrix products, arithmetic and copies ran while one was open for 0% of the time, Pallas kernels for 0%

profile of v2, /device:TPU:103, one launch (start us, length us, event | category | flops | bytes accessed | tf_op | source)
XLA Modules:
  0.0 453.2 jit_solution(1750129361742237372)
XLA Ops:
  0.0 0.9 convert_reduce_fusion.2
  0.9 0.6 scatter.4.c_ref
  1.5 15.0 %gather_counts.1 = f32[32,8,128]{2,1,0:T(8,128)} custom-call(f32[8,128]{1,0:T(8,128)} %scatter.4.c_ref), custom_call_target="tpu_custom_call" | custom-call | tf_op jit(solution)/shard_map/gather_counts/pallas_call | solution.py:80
  16.5 1.0 slice_reduce_fusion.4
  17.7 0.7 fusion.26
  19.2 1.3 fusion.27
  20.5 0.8 select_reduce_fusion.3
  21.3 0.7 broadcast_compare_fusion.1
  22.4 0.8 select_reduce_fusion.4
  23.2 3.5 broadcast_in_dim.201
  26.7 412.3 %while.29 = (s32[]{:T(128)}, f32[768,2048]{1,0:T(8,128)}, s32[]{:T(128)}, f32[768,2]{0,1:T(2,128)S(1)}, s32[768,2]{0,1:T(2,128)S(1)}, /*index=5*/s32[768,2]{0,1:...) while((s32[]{:T(128)}, f32[768,2048]{1,0:T(8,128)}, ...), condition=%wide.region_10.11_spmd, body=%wide.region_9.10_spmd.sunk | while | flops 34250182656 | bytes 200085344 | solution.py:405
  27.4 6.3 %fusion.72 = bf16[1280,2048]{1,0:T(8,128)(2,1)S(1)} fusion(bf16[768,2048]{1,0:T(8,128)(2,1)} %get-tuple-element.995, s32[768]{0:T(1024)S(1)} %get-tuple-element.934, s32[768]{0:T(1024)S(1)} %get-tuple-element.935), kind=kOutput, calls=%fused_computation.37.clone.1 | convolution fusion | flops 4029480960 | bytes 8394752 | tf_op jit(solution)/shard_map/while/body/dot_general | solution.py:344
  33.8 70.3 %all_to_all.18 = bf16[32,40,2048]{2,1,0:T(8,128)(2,1)S(1)} all-to-all(bf16[32,40,2048]{2,1,0:T(8,128)(2,1)S(1)} %bitcast.90), channel_id=1, replica_groups=mesh['dp'=1,'ep'=32] {'ep'}, dimensions={0} | all-to-all | bytes 10485760 | tf_op jit(solution)/shard_map/while/body/all_to_all | solution.py:380
  104.1 10.3 %fusion.73 = f32[1280,1408]{1,0:T(8,128)} fusion(bf16[1280,2048]{1,0:T(8,128)(2,1)S(1)} %bitcast.88, bf16[2048,1408]{1,0:T(8,128)(2,1)S(1)} %bitcast.81), kind=kOutput, calls=%fused_computation.80.clone.1 | convolution fusion | flops 7381975040 | bytes 18219008 | tf_op jit(solution)/shard_map/while/body/dot_general | solution.py:335
  114.4 24.6 %convolution_convert_fusion.2 = bf16[1280,2048]{1,0:T(8,128)(2,1)} fusion(bf16[1408,2048]{1,0:T(8,128)(2,1)} %get-tuple-element.998, bf16[1280,2048]{1,0:T(8,128)(2,1)} %bitcast.89, bf16[2048,1408]{1,0:T(8,128)(2,1)} %get-tuple-element.997, f32[1280,1408]{1,0:T(8,128)} %fusion.73), kind=kOutput, calls=%fused_computation.29.clone.1 | convolution fusion | flops 14777384960 | bytes 29229056 | tf_op jit(solution)/shard_map/while/body/dot_general | solution.py:338
  139.0 8.6 %all-to-all-start.1 = ((bf16[32,40,2048]{2,1,0:T(8,128)(2,1)}), bf16[32,40,2048]{2,1,0:T(8,128)(2,1)}, u32[]{:S(2)}, u32[]{:S(2)}) async-start(bf16[32,40,2048]{2,1,0:T(8,128)(2,1)} %bitcast.87), calls=%async_computation.1 | async-start | bytes 10485760 | tf_op jit(solution)/shard_map/while/body/all_to_all | solution.py:382
  147.6 69.2 %all-to-all-done.1 = bf16[32,40,2048]{2,1,0:T(8,128)(2,1)} async-done(((bf16[32,40,2048]{2,1,0:T(8,128)(2,1)}), bf16[32,40,2048]{2,1,0:T(8,128)(2,1)}, u32[]{:S(2)}, u32[]{:S(2)}) %all-to-all-start.1) | async-done | bytes 5242912 | tf_op jit(solution)/shard_map/while/body/all_to_all | solution.py:382
  216.8 6.4 %fusion.74 = f32[768,2048]{1,0:T(8,128)S(1)} fusion(bf16[1280,2048]{1,0:T(8,128)(2,1)} %bitcast.69, s32[768]{0:T(1024)S(1)} %get-tuple-element.935), kind=kOutput, calls=%fused_computation.35.clone.1 | convolution fusion | flops 4027514880 | bytes 11537408 | tf_op jit(solution)/shard_map/while/body/dot_general | solution.py:349
  223.2 8.7 %add_add_fusion.2 = f32[768,2048]{1,0:T(8,128)S(1)} fusion(f32[768,2048]{1,0:T(8,128)S(1)} %bitcast.76, f32[768,2048]{1,0:T(8,128)S(1)} %fusion.74, f32[768]{0:T(1024)S(1)} %get-tuple-element.936, f32[768]{0:T(1024)S(1)} %get-tuple-element.937, bf16[1280,2048]{1,0:T(8,128)(2,1)} %bitcast.69, s32[768]{0:T(1024)S(1)} %get-tuple-element.934), kind=kOutput, calls=%fused_computation.30.clone.1 | convolution fusion | flops 4033806336 | bytes 24126464 | tf_op jit(solution)/shard_map/while/body/dot_general | solution.py:350
  232.0 2.7 copy-done
  235.4 6.3 %fusion.72 = bf16[1280,2048]{1,0:T(8,128)(2,1)S(1)} fusion(bf16[768,2048]{1,0:T(8,128)(2,1)} %get-tuple-element.995, s32[768]{0:T(1024)S(1)} %get-tuple-element.934, s32[768]{0:T(1024)S(1)} %get-tuple-element.935), kind=kOutput, calls=%fused_computation.37.clone.1 | convolution fusion | flops 4029480960 | bytes 8394752 | tf_op jit(solution)/shard_map/while/body/dot_general | solution.py:344
  241.8 67.4 %all_to_all.18 = bf16[32,40,2048]{2,1,0:T(8,128)(2,1)S(1)} all-to-all(bf16[32,40,2048]{2,1,0:T(8,128)(2,1)S(1)} %bitcast.90), channel_id=1, replica_groups=mesh['dp'=1,'ep'=32] {'ep'}, dimensions={0} | all-to-all | bytes 10485760 | tf_op jit(solution)/shard_map/while/body/all_to_all | solution.py:380
  309.1 10.3 %fusion.73 = f32[1280,1408]{1,0:T(8,128)} fusion(bf16[1280,2048]{1,0:T(8,128)(2,1)S(1)} %bitcast.88, bf16[2048,1408]{1,0:T(8,128)(2,1)S(1)} %bitcast.81), kind=kOutput, calls=%fused_computation.80.clone.1 | convolution fusion | flops 7381975040 | bytes 18219008 | tf_op jit(solution)/shard_map/while/body/dot_general | solution.py:335
  319.5 24.6 %convolution_convert_fusion.2 = bf16[1280,2048]{1,0:T(8,128)(2,1)} fusion(bf16[1408,2048]{1,0:T(8,128)(2,1)} %get-tuple-element.998, bf16[1280,2048]{1,0:T(8,128)(2,1)} %bitcast.89, bf16[2048,1408]{1,0:T(8,128)(2,1)} %get-tuple-element.997, f32[1280,1408]{1,0:T(8,128)} %fusion.73), kind=kOutput, calls=%fused_computation.29.clone.1 | convolution fusion | flops 14777384960 | bytes 29229056 | tf_op jit(solution)/shard_map/while/body/dot_general | solution.py:338
  344.1 7.1 %all-to-all-start.1 = ((bf16[32,40,2048]{2,1,0:T(8,128)(2,1)}), bf16[32,40,2048]{2,1,0:T(8,128)(2,1)}, u32[]{:S(2)}, u32[]{:S(2)}) async-start(bf16[32,40,2048]{2,1,0:T(8,128)(2,1)} %bitcast.87), calls=%async_computation.1 | async-start | bytes 10485760 | tf_op jit(solution)/shard_map/while/body/all_to_all | solution.py:382
  351.2 69.2 %all-to-all-done.1 = bf16[32,40,2048]{2,1,0:T(8,128)(2,1)} async-done(((bf16[32,40,2048]{2,1,0:T(8,128)(2,1)}), bf16[32,40,2048]{2,1,0:T(8,128)(2,1)}, u32[]{:S(2)}, u32[]{:S(2)}) %all-to-all-start.1) | async-done | bytes 5242912 | tf_op jit(solution)/shard_map/while/body/all_to_all | solution.py:382
  420.4 6.4 %fusion.74 = f32[768,2048]{1,0:T(8,128)S(1)} fusion(bf16[1280,2048]{1,0:T(8,128)(2,1)} %bitcast.69, s32[768]{0:T(1024)S(1)} %get-tuple-element.935), kind=kOutput, calls=%fused_computation.35.clone.1 | convolution fusion | flops 4027514880 | bytes 11537408 | tf_op jit(solution)/shard_map/while/body/dot_general | solution.py:349
  426.8 8.7 %add_add_fusion.2 = f32[768,2048]{1,0:T(8,128)S(1)} fusion(f32[768,2048]{1,0:T(8,128)S(1)} %bitcast.76, f32[768,2048]{1,0:T(8,128)S(1)} %fusion.74, f32[768]{0:T(1024)S(1)} %get-tuple-element.936, f32[768]{0:T(1024)S(1)} %get-tuple-element.937, bf16[1280,2048]{1,0:T(8,128)(2,1)} %bitcast.69, s32[768]{0:T(1024)S(1)} %get-tuple-element.934), kind=kOutput, calls=%fused_computation.30.clone.1 | convolution fusion | flops 4033806336 | bytes 24126464 | tf_op jit(solution)/shard_map/while/body/dot_general | solution.py:350
  435.5 2.7 copy-done
  439.1 0.7 select_reduce_fusion.5
  439.9 8.4 %copy.32 = bf16[1,1408,2048]{1,2,0:T(8,128)(2,1)} copy(bf16[1,1408,2048]{2,1,0:T(8,128)(2,1)} %bitcast.92) | data formatting | bytes 11534336 | tf_op args[5]
  448.2 4.9 %convert_element_type.74 = bf16[768,2048]{1,0:T(8,128)(2,1)} convert(f32[768,2048]{1,0:T(8,128)} %get-tuple-element.583) | non-fusion elementwise | flops 1572864 | bytes 9437184 | tf_op jit(solution)/shard_map/convert_element_type | solution.py:407
  (53 shorter events, 0.9 us)
Async XLA Ops:
  0.0 26.7 %copy-start.3 = (s32[768,2]{0,1:T(2,128)S(1)}, s32[768,2]{0,1:T(2,128)}, u32[]{:S(2)}) copy-start(s32[768,2]{0,1:T(2,128)} %param.14) | copy-start | bytes 18436
  0.0 26.7 %copy-start.2 = (f32[768,2]{0,1:T(2,128)S(1)}, f32[768,2]{0,1:T(2,128)}, u32[]{:S(2)}) copy-start(f32[768,2]{0,1:T(2,128)} %param.15) | copy-start | bytes 18436
  17.6 9.1 %copy-start.7 = (s32[32]{0:T(128)}, s32[32]{0:T(128)S(1)}, u32[]{:S(2)}) copy-start(s32[32]{0:T(128)S(1)} %convert_reduce_fusion.3) | copy-start | bytes 388
  21.3 1.8 copy-start.5
  26.7 412.4 %copy-start.6 = (f32[768,2]{0,1:T(2,128)S(1)}, f32[768,2]{0,1:T(2,128)}, u32[]{:S(2)}) copy-start(f32[768,2]{0,1:T(2,128)} %copy-done.5) | copy-start | bytes 18436
  33.8 70.3 %slice-start.2 = ((s8[5767168]{0:T(1024)(128)(4,1)}), s8[4194304]{0:T(1024)(128)(4,1)S(1)}, s32[]{:S(2)}) async-start(s8[5767168]{0:T(1024)(128)(4,1)} %bitcast.80), calls=%async_computation.4 | async-start | bytes 8388608 | tf_op jit(solution)/shard_map/while
  33.8 70.3 %slice-start.3 = ((s8[5767168]{0:T(1024)(128)(4,1)}), s8[1572864]{0:T(1024)(128)(4,1)S(1)}, s32[]{:S(2)}) async-start(s8[5767168]{0:T(1024)(128)(4,1)} %bitcast.80), calls=%async_computation.5 | async-start | bytes 3145728 | tf_op jit(solution)/shard_map/while
  104.1 10.3 %copy-start.1 = (bf16[32,40,2048]{2,1,0:T(8,128)(2,1)}, bf16[32,40,2048]{2,1,0:T(8,128)(2,1)S(1)}, u32[]{:S(2)}) copy-start(bf16[32,40,2048]{2,1,0:T(8,128)(2,1)S(1)} %all_to_all.18) | copy-start | bytes 15728644 | tf_op jit(solution)/shard_map/while
  139.0 84.2 %slice-start = ((s8[6291456]{0:T(1024)(128)(4,1)}), s8[2097152]{0:T(1024)(128)(4,1)S(1)}, s32[]{:S(2)}) async-start(s8[6291456]{0:T(1024)(128)(4,1)} %bitcast.75), calls=%async_computation.2 | async-start | bytes 4194304 | tf_op jit(solution)/shard_map/while
  139.0 77.8 %all-to-all-start.1 = ((bf16[32,40,2048]{2,1,0:T(8,128)(2,1)}), bf16[32,40,2048]{2,1,0:T(8,128)(2,1)}, u32[]{:S(2)}, u32[]{:S(2)}) async-start(bf16[32,40,2048]{2,1,0:T(8,128)(2,1)} %bitcast.87), calls=%async_computation.1 | async-start | bytes 10485760 | tf_op jit(solution)/shard_map/while/body/all_to_all | solution.py:382
  216.8 6.4 %slice-start.1 = ((s8[6291456]{0:T(1024)(128)(4,1)}), s8[4194304]{0:T(1024)(128)(4,1)S(1)}, s32[]{:S(2)}) async-start(s8[6291456]{0:T(1024)(128)(4,1)} %bitcast.75), calls=%async_computation.3 | async-start | bytes 8388608 | tf_op jit(solution)/shard_map/while
  232.0 2.7 copy-start
  241.7 67.4 %slice-start.2 = ((s8[5767168]{0:T(1024)(128)(4,1)}), s8[4194304]{0:T(1024)(128)(4,1)S(1)}, s32[]{:S(2)}) async-start(s8[5767168]{0:T(1024)(128)(4,1)} %bitcast.80), calls=%async_computation.4 | async-start | bytes 8388608 | tf_op jit(solution)/shard_map/while
  241.8 67.4 %slice-start.3 = ((s8[5767168]{0:T(1024)(128)(4,1)}), s8[1572864]{0:T(1024)(128)(4,1)S(1)}, s32[]{:S(2)}) async-start(s8[5767168]{0:T(1024)(128)(4,1)} %bitcast.80), calls=%async_computation.5 | async-start | bytes 3145728 | tf_op jit(solution)/shard_map/while
  309.1 10.3 %copy-start.1 = (bf16[32,40,2048]{2,1,0:T(8,128)(2,1)}, bf16[32,40,2048]{2,1,0:T(8,128)(2,1)S(1)}, u32[]{:S(2)}) copy-start(bf16[32,40,2048]{2,1,0:T(8,128)(2,1)S(1)} %all_to_all.18) | copy-start | bytes 15728644 | tf_op jit(solution)/shard_map/while
  344.1 82.7 %slice-start = ((s8[6291456]{0:T(1024)(128)(4,1)}), s8[2097152]{0:T(1024)(128)(4,1)S(1)}, s32[]{:S(2)}) async-start(s8[6291456]{0:T(1024)(128)(4,1)} %bitcast.75), calls=%async_computation.2 | async-start | bytes 4194304 | tf_op jit(solution)/shard_map/while
  344.1 76.3 %all-to-all-start.1 = ((bf16[32,40,2048]{2,1,0:T(8,128)(2,1)}), bf16[32,40,2048]{2,1,0:T(8,128)(2,1)}, u32[]{:S(2)}, u32[]{:S(2)}) async-start(bf16[32,40,2048]{2,1,0:T(8,128)(2,1)} %bitcast.87), calls=%async_computation.1 | async-start | bytes 10485760 | tf_op jit(solution)/shard_map/while/body/all_to_all | solution.py:382
  420.4 6.4 %slice-start.1 = ((s8[6291456]{0:T(1024)(128)(4,1)}), s8[4194304]{0:T(1024)(128)(4,1)S(1)}, s32[]{:S(2)}) async-start(s8[6291456]{0:T(1024)(128)(4,1)} %bitcast.75), calls=%async_computation.3 | async-start | bytes 8388608 | tf_op jit(solution)/shard_map/while
  435.5 2.7 copy-start
  439.8 8.4 %copy-start.4 = (s32[4,16]{1,0:T(4,128)S(1)}, s32[4,16]{1,0:T(4,128)}, u32[]{:S(2)}) copy-start(s32[4,16]{1,0:T(4,128)} %constant.210.clone..sunk.3) | copy-start | bytes 772
